TPU v7x, 256 devices: a whole 4x4x8 slice. The times are simulated.
256 devices in a mesh: orig: 32 (over z, x), link: 8 (over y, core).
Axes of the slice: x: 4, y: 4, z: 8, core: 2. Of those that a mesh axis runs over, the one named last changes fastest.
Arguments:
- flows: float32 [3072], P('link'), may hold values from 0.2 to 2
- free_time: float32 [3072], P('link'), may hold values from 0.5 to 4
- capacity: float32 [3072], P('link'), may hold values from 0.5 to 2
- path_links: int32 [24, 1048576], P(None, ('orig', 'link')), may hold values from 0 to 3071, as said below
- demand: float32 [262144], P(('orig', 'link')), may hold values from 0.00012207031 to 0.0012207031
- chosen: int32 [262144], P(('orig', 'link')), may hold values from 0 to 3
Outputs:
- path_costs: float32 [1048576], P(('orig', 'link'))
- new_flows: float32 [3072], P('link')
Inputs may be any that keep to these rules, and one draw needn't show every extreme that they name: `path_links`: each entry is a link number; a path that names a link twice uses it twice. Pair k chooses path 4 * k + chosen[k].
All inputs are finite; a program needn't handle non-finite values.
Results may differ from a plain program's by a relative error of at most 0.00011.
Values sent between devices are 32-bit elements; how exact they have to be, the bound alone decides.
A program may use at most 128 MiB of HBM per device.

v0:
```python
import jax
import jax.numpy as jnp
from jax import lax
from jax.sharding import PartitionSpec as P

PER_OD = 4
LINE_STEPS = 8


def split_up(x, dim, peers):
    shape = x.shape
    pieces = x.reshape(*shape[:dim], peers, shape[dim] // peers, *shape[dim + 1 :])
    return jnp.moveaxis(pieces, dim, 0)


def sent_and_summed(x, axis, dim):
    peers = lax.axis_size(axis)
    pieces = lax.all_to_all(split_up(x, dim, peers), axis, 0, 0, tiled=True)
    return jnp.sum(pieces, axis=0)


def sent_to_all(x, axis):
    peers = lax.axis_size(axis)
    return lax.all_to_all(jnp.broadcast_to(x[None], (peers, *x.shape)), axis, 0, 0, tiled=True)


def taken_together(x, axis):
    everything = sent_to_all(x, axis)
    return jnp.sum(everything, axis=0)


def turned_gather(arrays, axis, dims):
    turned = [jnp.moveaxis(a, dim, 0) for a, dim in zip(arrays, dims)]
    widths = [t[0].size for t in turned]
    both = jnp.concatenate([t.reshape(-1, w) for t, w in zip(turned, widths)], axis=1)
    out = lax.all_gather(both, axis, axis=0, tiled=True)
    pieces = jnp.split(out, [sum(widths[:k]) for k in range(1, len(widths))], axis=1)
    return tuple(
        (
            jnp.moveaxis(b.reshape(-1, *t.shape[1:]), 0, dim)
            for b, t, dim in zip(pieces, turned, dims)
        )
    )


def travel(volume, free_time, capacity):
    ratio = volume / capacity
    square = ratio * ratio
    return free_time * (1.0 + 0.15 * square * square)


def link_counts(slots, count):
    link_ids = jnp.arange(count, dtype=jnp.int32)
    hits = slots[:, None, :] == link_ids[None, :, None]
    return jnp.sum(hits.astype(jnp.float32), axis=0)


def line_search(flows, direction, free_time, capacity, reducer):
    alpha = jnp.float32(0.5)
    for step in range(LINE_STEPS):
        volume = flows + alpha * direction
        ratio = volume / capacity
        square = ratio * ratio
        slope = jnp.sum(free_time * (1.0 + 0.15 * square * square) * direction)
        curve = jnp.sum(
            free_time / capacity * direction * direction * (1.0 + 0.6 * square * square)
        )
        slope, curve = reducer(slope, curve)
        alpha = alpha - slope / curve
    return alpha


def local(flows, free_time, capacity, path_links, demand, chosen):
    link_dev = flows.shape[0]
    times = travel(flows, free_time, capacity)
    piece = lax.all_gather(times, "link", axis=0, tiled=True)
    counts = link_counts(path_links, piece.shape[0])
    path_costs = jnp.dot(piece, counts, precision=lax.Precision.HIGHEST)
    grouped = path_links.reshape(path_links.shape[0], -1, PER_OD)
    candidate = jnp.arange(PER_OD, dtype=jnp.int32)
    picker = (chosen[:, None] == candidate[None, :]).astype(jnp.int32)
    picked = jnp.sum(grouped * picker[None, :, :], axis=2)
    counts = link_counts(picked, link_dev * lax.axis_size("link"))
    owned = sent_and_summed(jnp.dot(counts, demand, precision=lax.Precision.HIGHEST), "link", 0)
    loads = taken_together(owned, "orig")
    direction = loads - flows
    every_flow, every_step, every_time, every_cap = turned_gather(
        (flows, direction, free_time, capacity), "link", (0, 0, 0, 0)
    )

    def keep_local(first, second):
        return (first, second)

    alpha = line_search(every_flow, every_step, every_time, every_cap, keep_local)
    new_flows = flows + alpha * direction
    return (path_costs, new_flows)


def solution(mesh):
    return jax.shard_map(
        local,
        mesh=mesh,
        in_specs=(
            P("link"),
            P("link"),
            P("link"),
            P(None, ("orig", "link")),
            P(("orig", "link")),
            P(("orig", "link")),
        ),
        out_specs=(P(("orig", "link")), P("link")),
        check_vma=False,
    )
```

profile of v0, /device:TPU:1, one launch (start us, length us, event | category | flops | bytes accessed | tf_op | source)
XLA Modules:
  0.0 328.2 jit_solution(9804823357907077979)
XLA Ops:
  0.6 0.0 copy-start
  0.6 0.0 copy-start.3
  0.7 0.0 copy-start.2
  0.7 0.0 copy-start.1
  0.7 0.9 fusion
  1.6 1.6 copy.13
  3.2 5.8 %multiply_reduce_fusion = s32[24,1024]{0,1:T(8,128)S(1)} fusion(s32[24,1024,4]{0,2,1:T(4,128)S(1)} %bitcast.20, s32[1024,4]{1,0:T(8,128)S(1)} %fusion), kind=kLoop, calls=%fused_computation.4 | loop fusion | flops 172032 | bytes 507904 | tf_op jit(solution)/shard_map/reduce_sum | solution.py:82
  9.0 0.2 copy.14
  9.2 47.2 %convert_reduce_fusion.1 = f32[3072,1024]{1,0:T(8,128)} fusion(s32[24,1024]{1,0:T(8,128)S(1)} %copy.14), kind=kLoop, calls=%fused_computation.2 | loop fusion | flops 223346688 | bytes 12681216 | tf_op jit(solution)/shard_map/reduce_sum | solution.py:55
  56.4 0.0 copy-done
  56.4 13.4 %fusion.61 = f32[1,8,384]{2,0,1:T(1,128)S(1)} fusion(f32[8,384,1024]{2,1,0:T(8,128)} %bitcast.19, f32[1024,1,1]{0,1,2:T(1,128)S(1)} %bitcast.18), kind=kOutput, calls=%fused_computation.96 | convolution fusion | flops 37748736 | bytes 12599296 | tf_op jit(solution)/shard_map/dot_general | solution.py:84
  69.9 10.4 %all_to_all.15 = f32[8,1,384]{2,1,0:T(1,128)S(1)} all-to-all(f32[8,1,384]{2,1,0:T(1,128)S(1)} %all_to_all.10), channel_id=1, replica_groups=mesh['orig'=32,'link'=8] {'link'}, dimensions={0} | all-to-all | bytes 24576 | tf_op jit(solution)/shard_map/all_to_all | solution.py:18
  80.3 0.6 broadcast_in_dim.2
  80.9 11.0 %all-to-all-start.1 = ((f32[32,1,384]{2,1,0:T(1,128)}), f32[32,1,384]{2,1,0:T(1,128)S(1)}, u32[]{:S(2)}, u32[]{:S(2)}) async-start(f32[32,1,384]{2,1,0:T(1,128)} %broadcast_in_dim.2), calls=%async_computation.1 | async-start | bytes 98304 | tf_op jit(solution)/shard_map/all_to_all | solution.py:24
  92.0 166.5 %convert_reduce_fusion = f32[3072,4096]{1,0:T(8,128)} fusion(s32[24,4096]{1,0:T(8,128)} %param.9), kind=kLoop, calls=%fused_computation | loop fusion | flops 893386752 | bytes 50724864 | tf_op jit(solution)/shard_map/reduce_sum | solution.py:55
  258.4 0.0 copy-done.3
  258.4 0.0 copy-done.2
  258.5 0.0 copy-done.1
  258.5 0.0 all-to-all-done.1
  258.5 0.1 reduce_sum.193
  258.6 13.7 %all_gather.7 = f32[3072,4]{0,1:T(4,128)S(1)} all-gather(f32[384,4]{0,1:T(4,128)S(1)} %pad_maximum_fusion), channel_id=1, replica_groups=mesh['orig'=32,'link'=8] {'link'}, dimensions={0}, use_global_device_ids=true | all-gather | bytes 55296 | tf_op jit(solution)/shard_map/all_gather | solution.py:36
  272.3 0.6 fusion.7
  274.3 0.6 fusion.14
  276.2 0.6 fusion.21
  278.2 0.6 fusion.28
  280.1 0.6 fusion.35
  282.1 0.6 fusion.42
  284.1 0.6 fusion.49
  286.0 0.6 fusion.56
  288.0 0.6 multiply_add_fusion
  288.6 11.4 %all-gather = f32[8,1,384]{2,1,0:T(1,128)S(1)} all-gather(f32[1,1,384]{2,1,0:T(1,128)S(1)} %reshape.71), channel_id=1, replica_groups=mesh['orig'=32,'link'=8] {'link'}, dimensions={0}, use_global_device_ids=true | all-gather | bytes 13824 | tf_op jit(solution)/shard_map/all_gather | solution.py:76
  300.0 28.2 %fusion.60 = f32[1,4096]{1,0:T(1,128)} fusion(f32[3072,1]{0,1:T(1,128)S(1)} %bitcast.53, f32[3072,4096]{1,0:T(8,128)} %convert_reduce_fusion), kind=kOutput, calls=%fused_computation.95 | convolution fusion | flops 150994944 | bytes 50360320 | tf_op jit(solution)/shard_map/dot_general | solution.py:78
  (11 shorter events, 0.1 us)
Async XLA Ops:
  0.6 55.8 %copy-start = (f32[1024]{0:T(1024)S(1)}, f32[1024]{0:T(1024)}, u32[]{:S(2)}) copy-start(f32[1024]{0:T(1024)} %param.10) | copy-start | bytes 12292
  0.6 257.8 %copy-start.3 = (f32[384]{0:T(512)S(1)}, f32[384]{0:T(512)}, u32[]{:S(2)}) copy-start(f32[384]{0:T(512)} %param.7) | copy-start | bytes 4612
  0.7 257.8 %copy-start.2 = (f32[384]{0:T(512)S(1)}, f32[384]{0:T(512)}, u32[]{:S(2)}) copy-start(f32[384]{0:T(512)} %param.8) | copy-start | bytes 4612
  0.7 257.8 %copy-start.1 = (f32[384]{0:T(512)S(1)}, f32[384]{0:T(512)}, u32[]{:S(2)}) copy-start(f32[384]{0:T(512)} %param.6) | copy-start | bytes 4612
  80.9 177.6 %all-to-all-start.1 = ((f32[32,1,384]{2,1,0:T(1,128)}), f32[32,1,384]{2,1,0:T(1,128)S(1)}, u32[]{:S(2)}, u32[]{:S(2)}) async-start(f32[32,1,384]{2,1,0:T(1,128)} %broadcast_in_dim.2), calls=%async_computation.1 | async-start | bytes 98304 | tf_op jit(solution)/shard_map/all_to_all | solution.py:24
where the time goes:
time: 329 us; the launch traced here: 328 us
  other arithmetic  226 us (69%)
  matrix products  41.6 us (13%)
  blocking collectives  35.5 us (11%)
  between operations  11.5 us (3%)
  starting transfers between devices  11 us (3%)
    reduce_sum x2, other arithmetic, link_counts(): return jnp.sum(hits.astype(jnp.float32), axis=0)  214 us
    dot_general x1, matrix products, local(): path_costs = jnp.dot(piece, counts, precision=lax.Precision.HIGHEST)  28.2 us
    all_gather x1, blocking collectives, turned_gather(): out = lax.all_gather(both, axis, axis=0, tiled=True)  13.7 us
    dot_general x1, matrix products, local(): jnp.dot(counts, demand, precision=lax.Precision.HIGHEST)  13.4 us
    all_gather x1, blocking collectives, local(): piece = lax.all_gather(times, 'link', axis=0, tiled=True)  11.4 us
    all_to_all x1, starting transfers between devices, sent_to_all(): lax.all_to_all(jnp.broadcast_to(x[None], (peers, *x.shape)), axis, 0, 0,...  11 us
    all_to_all x1, blocking collectives, sent_and_summed(): pieces = lax.all_to_all(split_up(x, dim, peers), axis, 0, 0, tiled=True)  10.4 us
  transfers between devices with their start and end apart: 1, of which 0 were waited for; matrix products, arithmetic and copies ran while one was open for 51% of the time, Pallas kernels for 0%

commit v1 on v0

v1 whole, which is shorter than its diff:
```python
import functools

import jax
import jax.numpy as jnp
from jax import lax
from jax.experimental import pallas as pl
from jax.experimental.pallas import tpu as pltpu
from jax.sharding import PartitionSpec as P

PER_OD = 4
LINE_STEPS = 8
LANES = 128
MESH = pl.DeviceIdType.MESH


def travel(volume, free_time, capacity):
    ratio = volume / capacity
    square = ratio * ratio
    return free_time * (1.0 + 0.15 * square * square)


def gathered(table, index):
    return jnp.take_along_axis(table, index, axis=1, mode="promise_in_bounds")


def kernel(
    links_hbm,
    chosen_hbm,
    demand_hbm,
    flows_hbm,
    free_hbm,
    cap_hbm,
    costs_ref,
    new_ref,
    links,
    chosen,
    demand,
    flows,
    free,
    cap,
    part,
    recv,
    sums,
    terms,
    table,
    local_sem,
    time_send,
    time_recv,
    part_send,
    part_recv,
    sum_send,
    sum_recv,
    term_send,
    term_recv,
):
    hops, paths = links.shape
    rows = table.shape[1]
    n_link = table.shape[0]
    n_orig = sums.shape[0]
    n_rows = n_link * rows
    me_link = lax.axis_index("link")
    me_orig = lax.axis_index("orig")

    loads_in = [
        pltpu.make_async_copy(src, dst, local_sem.at[k])
        for k, (src, dst) in enumerate(
            (
                (chosen_hbm, chosen),
                (links_hbm, links),
                (demand_hbm, demand),
                (flows_hbm, flows),
                (free_hbm, free),
                (cap_hbm, cap),
            )
        )
    ]
    for copy in loads_in:
        copy.start()

    barrier = pltpu.get_barrier_semaphore()
    for d in range(1, n_link):
        pl.semaphore_signal(
            barrier, inc=1, device_id=(me_orig, (me_link + d) % n_link), device_id_type=MESH
        )
    for d in range(1, n_orig):
        pl.semaphore_signal(
            barrier, inc=1, device_id=((me_orig + d) % n_orig, me_link), device_id_type=MESH
        )

    for copy in loads_in:
        copy.wait()

    table[me_link] = travel(flows[...], free[...], cap[...])

    lane = lax.broadcasted_iota(jnp.int32, (8, LANES), 1)
    quarter = lane // (LANES // PER_OD)
    first = (lane * PER_OD) % LANES
    low_ids = lax.broadcasted_iota(jnp.int32, (LANES, LANES), 0).astype(jnp.int16)
    row_ids = lax.broadcasted_iota(jnp.int32, (2 * n_rows, LANES), 0)
    coarse = row_ids < n_rows
    high_ids = jnp.where(coarse, row_ids, row_ids - n_rows).astype(jnp.int16)

    def block(b, total):
        start = pl.multiple_of(b * (PER_OD * LANES), PER_OD * LANES)
        where_to = first + chosen[pl.ds(b, 1), :]
        weight = demand[pl.ds(b, 1), :]
        upper = weight.astype(jnp.bfloat16).astype(jnp.float32)
        both = jnp.where(coarse, upper, weight - upper).astype(jnp.bfloat16)
        picked = []
        for g in range(hops // 8):
            group = None
            for q in range(PER_OD):
                found = gathered(
                    links[8 * g : 8 * g + 8, pl.ds(start + q * LANES, LANES)], where_to
                )
                group = found if q == 0 else jnp.where(quarter == q, found, group)
            picked.append(group)
        picked = jnp.concatenate(picked, axis=0)
        high = picked // LANES
        low = picked % LANES
        for h in range(0, hops, 2):
            lefts, rights = [], []
            for k in (h, h + 1):
                hi = jnp.broadcast_to(high[k : k + 1], (2 * n_rows, LANES)).astype(jnp.int16)
                lo = jnp.broadcast_to(low[k : k + 1], (LANES, LANES)).astype(jnp.int16)
                lefts.append(jnp.where(hi == high_ids, both, jnp.bfloat16(0)))
                rights.append(
                    jnp.where(lo == low_ids, jnp.bfloat16(1), jnp.bfloat16(0))
                )
            total = total + lax.dot_general(
                jnp.concatenate(lefts, axis=1),
                jnp.concatenate(rights, axis=1),
                (((1,), (1,)), ((), ())),
                preferred_element_type=jnp.float32,
            )
        return total

    total = lax.fori_loop(
        0,
        chosen.shape[0],
        block,
        jnp.zeros((2 * n_rows, LANES), jnp.float32),
    )
    total = total[:n_rows] + total[n_rows:]
    for k in range(n_link):
        part[k] = total[k * rows : (k + 1) * rows]

    pl.semaphore_wait(barrier, n_link + n_orig - 2)

    def to_link(src, dst, send, recv_sem, d):
        return pltpu.make_async_remote_copy(
            src_ref=src,
            dst_ref=dst,
            send_sem=send.at[d],
            recv_sem=recv_sem.at[d],
            device_id=(me_orig, (me_link + d) % n_link),
            device_id_type=MESH,
        )

    waits = []
    part_copies = [
        to_link(part.at[(me_link + d) % n_link], recv.at[me_link], part_send, part_recv, d)
        for d in range(1, n_link)
    ]
    time_copies = [
        to_link(table.at[me_link], table.at[me_link], time_send, time_recv, d)
        for d in range(1, n_link)
    ]
    for copy in part_copies:
        copy.start()
    for copy in time_copies:
        copy.start()
    recv[me_link] = part[me_link]
    for copy in part_copies:
        copy.wait_recv()
    partial = recv[0]
    for k in range(1, n_link):
        partial = partial + recv[k]
    sums[me_orig] = partial

    sum_copies = [
        pltpu.make_async_remote_copy(
            src_ref=sums.at[me_orig],
            dst_ref=sums.at[me_orig],
            send_sem=sum_send.at[d],
            recv_sem=sum_recv.at[d],
            device_id=((me_orig + d) % n_orig, me_link),
            device_id_type=MESH,
        )
        for d in range(1, n_orig)
    ]
    for copy in sum_copies:
        copy.start()

    for copy in time_copies:
        copy.wait_recv()
    times = [
        jnp.broadcast_to(table[r // rows, pl.ds(r % rows, 1), :], (8, LANES))
        for r in range(n_rows)
    ]

    def costs(b, carry):
        start = pl.multiple_of(b * LANES, LANES)
        total = jnp.zeros((8, LANES), jnp.float32)
        for g in range(hops // 8):
            index = links[8 * g : 8 * g + 8, pl.ds(start, LANES)]
            high = index // LANES
            low = index % LANES
            value = gathered(times[0], low)
            for r in range(1, n_rows):
                value = jnp.where(high == r, gathered(times[r], low), value)
            total = total + value
        costs_ref[pl.ds(b, 1), :] = jnp.sum(total, axis=0, keepdims=True)
        return carry

    lax.fori_loop(0, paths // LANES, costs, 0)

    for copy in sum_copies:
        copy.wait_recv()
    loads = sums[0]
    for k in range(1, n_orig):
        loads = loads + sums[k]
    flow = flows[...]
    direction = loads - flow

    inverse = 1.0 / cap[...]
    p = flow * inverse
    q = direction * inverse
    pp, pq, qq = p * p, p * q, q * q
    powers = (pp * pp, 4.0 * pp * pq, 6.0 * pp * qq, 4.0 * pq * qq, qq * qq)
    slope_one = free[...] * direction
    curve_one = slope_one * q
    coefficients = []
    for one, factor in ((slope_one, 0.15), (curve_one, 0.6)):
        scaled = factor * one
        for k, power in enumerate(powers):
            term = scaled * power
            coefficients.append(one + term if k == 0 else term)
    spot = lax.broadcasted_iota(jnp.int32, (rows, LANES), 1)
    packed = jnp.zeros((rows, LANES), jnp.float32)
    for k, term in enumerate(coefficients):
        packed = jnp.where(spot == k, jnp.sum(term, axis=1, keepdims=True), packed)
    terms[me_link] = packed
    term_copies = [
        to_link(terms.at[me_link], terms.at[me_link], term_send, term_recv, d)
        for d in range(1, n_link)
    ]
    for copy in term_copies:
        copy.start()
    for copy in part_copies + time_copies + sum_copies:
        copy.wait_send()
    for copy in term_copies:
        copy.wait_recv()
    whole = terms[0]
    for k in range(1, n_link):
        whole = whole + terms[k]
    whole = jnp.sum(whole, axis=0, keepdims=True)
    count = len(coefficients)
    c = [
        jnp.sum(jnp.where(spot[:1] == k, whole, 0.0), axis=1, keepdims=True)
        for k in range(count)
    ]
    s, u = c[: count // 2], c[count // 2 :]
    alpha = jnp.full((1, 1), 0.5, jnp.float32)
    for step in range(LINE_STEPS):
        slope, curve = s[-1], u[-1]
        for k in range(len(s) - 2, -1, -1):
            slope = slope * alpha + s[k]
            curve = curve * alpha + u[k]
        alpha = alpha - slope / curve
    new_ref[...] = flow + alpha * direction
    for copy in term_copies:
        copy.wait_send()


def local(n_orig, n_link, flows, free_time, capacity, path_links, demand, chosen):
    rows = flows.shape[0] // LANES
    hops, paths = path_links.shape
    pairs = demand.shape[0] // LANES
    f32 = jnp.float32
    any_space = pl.BlockSpec(memory_space=pl.ANY)
    vmem = pl.BlockSpec(memory_space=pltpu.VMEM)
    dma = pltpu.SemaphoreType.DMA
    costs, new = pl.pallas_call(
        kernel,
        out_shape=(
            jax.ShapeDtypeStruct((paths // LANES, LANES), f32),
            jax.ShapeDtypeStruct((rows, LANES), f32),
        ),
        in_specs=[any_space] * 6,
        out_specs=(vmem, vmem),
        scratch_shapes=[
            pltpu.VMEM((hops, paths), jnp.int32),
            pltpu.VMEM((pairs, LANES), jnp.int32),
            pltpu.VMEM((pairs, LANES), f32),
            pltpu.VMEM((rows, LANES), f32),
            pltpu.VMEM((rows, LANES), f32),
            pltpu.VMEM((rows, LANES), f32),
            pltpu.VMEM((n_link, rows, LANES), f32),
            pltpu.VMEM((n_link, rows, LANES), f32),
            pltpu.VMEM((n_orig, rows, LANES), f32),
            pltpu.VMEM((n_link, rows, LANES), f32),
            pltpu.VMEM((n_link, rows, LANES), f32),
            dma((6,)),
            dma((n_link,)),
            dma((n_link,)),
            dma((n_link,)),
            dma((n_link,)),
            dma((n_orig,)),
            dma((n_orig,)),
            dma((n_link,)),
            dma((n_link,)),
        ],
        compiler_params=pltpu.CompilerParams(collective_id=0, has_side_effects=True),
    )(
        path_links,
        chosen.reshape(pairs, LANES),
        demand.reshape(pairs, LANES),
        flows.reshape(rows, LANES),
        free_time.reshape(rows, LANES),
        capacity.reshape(rows, LANES),
    )
    return costs.reshape(paths), new.reshape(rows * LANES)


def solution(mesh):
    return jax.shard_map(
        functools.partial(local, mesh.shape["orig"], mesh.shape["link"]),
        mesh=mesh,
        in_specs=(
            P("link"),
            P("link"),
            P("link"),
            P(None, ("orig", "link")),
            P(("orig", "link")),
            P(("orig", "link")),
        ),
        out_specs=(P(("orig", "link")), P("link")),
        check_vma=False,
    )
```

time: 329 us -> 30.1 us (0.09)
  other arithmetic: 226 us -> 0 us
  matrix products: 41.6 us -> 0 us
  blocking collectives: 35.5 us -> 0 us
  Pallas kernels: 0 us -> 27.4 us
  starting transfers between devices: 11 us -> 0 us
  between operations: 11.5 us -> 0.65 us
    reduce_sum x13 -> x0, other arithmetic: 225 us -> none  [the longest x2 214 us: link_counts(): return jnp.sum(hits.astype(jnp.float32), axis=0)]
    dot_general x2 -> x0, matrix products: 41.6 us -> none  [the longest x1 28.2 us: local(): path_costs = jnp.dot(piece, counts, precision=lax.Precision.HIGHEST)]
    pallas_call x0 -> x1, Pallas kernels: none -> 27.4 us  [local(): pl.pallas_call(kernel, out_shape=(jax.ShapeDtypeStruct((paths // LANES, L...]
    all_gather x2 -> x0, blocking collectives: 25.1 us -> none  [the longest x1 13.7 us: turned_gather(): out = lax.all_gather(both, axis, axis=0, tiled=True)]
    all_to_all x1 -> x0, starting transfers between devices: 11 us -> none  [sent_to_all(): lax.all_to_all(jnp.broadcast_to(x[None], (peers, *x.shape)), axis, 0, 0,...]
    all_to_all x1 -> x0, blocking collectives: 10.4 us -> none  [sent_and_summed(): pieces = lax.all_to_all(split_up(x, dim, peers), axis, 0, 0, tiled=True)]
  transfers between devices with their start and end apart: 1 -> 0, of which waited for: 0 -> 0; matrix products, arithmetic and copies ran while one was open for 51% -> 0% of each run, Pallas kernels for 0% -> 0%
where the time goes in v1:
time: 30.1 us; the launch traced here: 30 us
  Pallas kernels  27.4 us (91%)
  local copies, waits for them, and re-layouts  1.91 us (6%)
  between operations  0.65 us (2%)
    pallas_call x1, Pallas kernels, local(): pl.pallas_call(kernel, out_shape=(jax.ShapeDtypeStruct((paths // LANES, L...  27.4 us
    unnamed x4, local copies, waits for them, and re-layouts  1.91 us

profile of v1, /device:TPU:1, one launch (start us, length us, event | category | flops | bytes accessed | tf_op | source)
XLA Modules:
  0.0 30.0 jit_solution(6286073614263236144)
XLA Ops:
  0.6 27.4 %shard_map.77 = (f32[32,128]{1,0:T(8,128)}, f32[3,128]{1,0:T(4,128)}) custom-call(s32[24,4096]{1,0:T(8,128)} %links_hbm.1, s32[8,128]{1,0:T(8,128)} %bitcast.8, f32[8,128]{1,0:T(8,128)} %bitcast.9, f32[3,128]{1,0:T(4,128)} %bitcast.10, f32[3,128]{1,0:T(4,128)} %bitcast.11, f32[3,128]{1,0:T(4,128)} %bitcast.12), custom_call_target="tpu_custom_call" | custom-call | tf_op jit(solution)/shard_map/pallas_call | solution.py:284
  28.1 0.0 copy-start
  28.1 1.3 %copy.10 = f32[4096]{0:T(1024)} copy(f32[4096]{0:T(1024)} %bitcast.7) | data formatting | bytes 32768
  29.4 0.0 copy-done
  29.4 0.6 %copy.11 = f32[384]{0:T(512)} copy(f32[384]{0:T(512)S(1)} %bitcast.13) | data formatting | bytes 3072
Async XLA Ops:
  28.1 1.3 %copy-start = (f32[3,128]{1,0:T(4,128)S(1)}, f32[3,128]{1,0:T(4,128)}, u32[]{:S(2)}) copy-start(f32[3,128]{1,0:T(4,128)} %get-tuple-element.5) | copy-start | bytes 4612
